TPU v7x, 128 devices: a whole 4x4x4 slice. The times are simulated.
128 devices in a mesh: dp: 4 (over z_hi, core), seq: 32 (over y, z_lo, x).
Axes of the slice: x: 4, y: 4, z: 4 (z_hi: 2, z_lo: 2; z = z_hi * 2 + z_lo), core: 2. Of those that a mesh axis runs over, the one named last changes fastest.
Arguments:
- spectrum: bfloat16 [40960, 128], P(('dp', 'seq')), parts along dimension 0, may hold values from -7 to 7
- valid_frames: int32 [4], P('dp'), parts along dimension 0, may hold values from 1280 to 5120
- inlet_weight: bfloat16 [3, 128, 1280], replicated, may hold values from -0.3125 to 0.3125
- inlet_bias: float32 [1280], replicated, may hold values from -3 to 3
- stride_weight: bfloat16 [3, 1280, 1280], replicated, may hold values from -0.09375 to 0.09375
- stride_bias: float32 [1280], replicated, may hold values from -3 to 3
- norm_gain: float32 [1280], replicated, may hold values from 0.1 to 1.9
- norm_bias: float32 [1280], replicated, may hold values from -3 to 3
- projection_weight: bfloat16 [1280, 3840], replicated, may hold values from -1.2018865 to 1.2018865
- query_value_bias: float32 [2, 1280], replicated, may hold values from -5 to 5
- out_weight: bfloat16 [1280, 1280], replicated, may hold values from -0.15625 to 0.15625
- out_bias: float32 [1280], replicated, may hold values from -3 to 3
Outputs:
- attended: bfloat16 [20480, 1280], P(('dp', 'seq')), parts along dimension 0
- encoded: bfloat16 [20480, 1280], P(('dp', 'seq')), parts along dimension 0
There are 4 independent parts, one for each index of `dp`. A program takes and returns all parts, laid end to end along the dimension named above; an argument that names none is the same for every part. Nothing has to cross between parts.
Inputs may be any that keep to these rules, and one draw needn't show every extreme that they name: Frames from valid_frames[0] on are padding and are never used as keys.
All inputs are finite; a program needn't handle non-finite values.
Results may differ from a plain program's by a relative error of at most 0.033.
Values may be sent and summed in bfloat16 or wider, within the bound.
No kernel may reach another device: no remote copies, remote signals or barrier semaphores. Data moves between devices by JAX's collectives and lax.ppermute only.
A program may use at most 256 MiB of HBM per device.

v0:
```python
import math

import jax
import jax.numpy as jnp
from jax import lax
from jax.sharding import PartitionSpec as P

HEAD_DIM = 64


masked_score = -1e30
norm_epsilon = 1e-05


def extended(cells, sides, width):
    for axis, dim in sides:
        count = lax.axis_size(axis)
        ends = count - 1
        head = lax.slice_in_dim(cells, 0, width, axis=dim)
        tail = lax.slice_in_dim(cells, cells.shape[dim] - width, cells.shape[dim], axis=dim)
        cells = jnp.concatenate(
            [
                lax.ppermute(tail, axis, [(i, (i + 1) % count) for i in range(ends)]),
                cells,
                lax.ppermute(head, axis, [((i + 1) % count, i) for i in range(ends)]),
            ],
            axis=dim,
        )
    return cells


def gelu_exact(inputs):
    return jax.nn.gelu(inputs, approximate=False)


def sinusoids(first_frame, frame_count, model_width):
    half_width = model_width // 2
    increment = math.log(10000.0) / (half_width - 1)
    inverse = jnp.exp(-increment * jnp.arange(half_width, dtype=jnp.float32))
    moments = (first_frame + jnp.arange(frame_count, dtype=jnp.int32)).astype(jnp.float32)
    angles = moments[:, None] * inverse[None, :]
    return jnp.concatenate([jnp.sin(angles), jnp.cos(angles)], axis=1)


def shards(
    spectrum,
    valid_frames,
    inlet_weight,
    inlet_bias,
    stride_weight,
    stride_bias,
    norm_gain,
    norm_bias,
    projection_weight,
    query_value_bias,
    out_weight,
    out_bias,
):
    mel_rows = spectrum.shape[0]
    frames = mel_rows // 2
    channels = spectrum.shape[1]
    model_width = projection_weight.shape[0]
    head_count = model_width // HEAD_DIM
    device_index = lax.axis_index("seq")
    inlet_matrix = inlet_weight.reshape(3 * channels, model_width)
    widened = extended(spectrum, (("seq", 0),), 2)
    stacked = jnp.concatenate(
        [widened[0 : mel_rows + 1], widened[1 : mel_rows + 2], widened[2 : mel_rows + 3]], axis=1
    )
    activated = gelu_exact(
        jnp.dot(stacked, inlet_matrix, preferred_element_type=jnp.float32) + inlet_bias
    )
    leading = jnp.logical_and(device_index == 0, jnp.arange(mel_rows + 1, dtype=jnp.int32) == 0)
    first_conv = jnp.where(leading[:, None], 0.0, activated).astype(jnp.bfloat16)
    paired = first_conv[0:mel_rows].reshape(frames, 2, model_width)
    stacked_two = jnp.concatenate([paired[:, 0], paired[:, 1], first_conv[2::2]], axis=1)
    second_conv = gelu_exact(
        jnp.dot(
            stacked_two,
            stride_weight.reshape(3 * model_width, model_width),
            preferred_element_type=jnp.float32,
        )
        + stride_bias
    )
    stem_out = (second_conv + sinusoids(device_index * frames, frames, model_width)).astype(
        jnp.bfloat16
    )
    widened_stem = stem_out.astype(jnp.float32)
    centre = jnp.mean(widened_stem, axis=1, keepdims=True)
    spread = jnp.mean((widened_stem - centre) ** 2, axis=1, keepdims=True)
    normed = (
        (widened_stem - centre) * lax.rsqrt(spread + norm_epsilon) * norm_gain + norm_bias
    ).astype(jnp.bfloat16)
    projected = jnp.dot(normed, projection_weight, preferred_element_type=jnp.float32)
    queries = (projected[:, 0:model_width] + query_value_bias[0]).astype(jnp.bfloat16)
    key_rows = projected[:, model_width : 2 * model_width].astype(jnp.bfloat16)
    values = (projected[:, 2 * model_width : 3 * model_width] + query_value_bias[1]).astype(
        jnp.bfloat16
    )
    live_count = valid_frames[0]
    scaling = HEAD_DIM ** (-0.5)
    query_heads = queries.reshape(frames, head_count, HEAD_DIM)
    highest = jnp.full((frames, head_count), masked_score, jnp.float32)
    summed = jnp.zeros((frames, model_width), jnp.float32)
    key_piece = lax.all_gather(key_rows, "seq", axis=0, tiled=True)
    value_piece = lax.all_gather(values, "seq", axis=0, tiled=True)
    piece_rows = key_piece.shape[0]
    key_live = jnp.arange(piece_rows, dtype=jnp.int32) < live_count
    scores = (
        jnp.einsum(
            "qhd,khd->qhk",
            query_heads,
            key_piece.reshape(piece_rows, head_count, HEAD_DIM),
            preferred_element_type=jnp.float32,
        )
        * scaling
    )
    scores = jnp.where(key_live[None, None, :], scores, masked_score)
    new_highest = jnp.maximum(highest, jnp.max(scores, axis=2))
    weights = jnp.where(key_live[None, None, :], jnp.exp(scores - new_highest[:, :, None]), 0.0)
    retain = jnp.exp(highest - new_highest)
    totals = jnp.sum(weights, axis=2)
    partial_value = jnp.einsum(
        "qhk,khd->qhd",
        weights.astype(jnp.bfloat16),
        value_piece.reshape(piece_rows, head_count, HEAD_DIM),
        preferred_element_type=jnp.float32,
    )
    summed = summed * jnp.repeat(retain, HEAD_DIM, axis=1) + partial_value.reshape(
        frames, model_width
    )
    highest, totals, summed = (new_highest, totals, summed)
    mixed_rows = (summed / jnp.repeat(totals, HEAD_DIM, axis=1)).astype(jnp.bfloat16)
    output = jnp.dot(mixed_rows, out_weight, preferred_element_type=jnp.float32) + out_bias
    return (output.astype(jnp.bfloat16), (widened_stem + output).astype(jnp.bfloat16))


def solution(mesh):
    in_specs = (P(("dp", "seq"), None), P("dp"), P(), P(), P(), P(), P(), P(), P(), P(), P(), P())
    out_specs = (P(("dp", "seq"), None), P(("dp", "seq"), None))
    return jax.shard_map(shards, mesh=mesh, in_specs=in_specs, out_specs=out_specs, check_vma=False)
```

profile of v0, /device:TPU:0, one launch (start us, length us, event | category | flops | bytes accessed | tf_op | source)
XLA Modules:
  0.0 461.2 jit_solution(16095405119642262128)
XLA Ops:
  7.2 0.9 fusion.74
  8.1 3.6 collective-permute-start
  11.7 1.3 collective-permute-start.1
  13.1 2.4 multiply_sine_fusion
  15.4 0.9 slice_maximum_fusion
  16.4 0.8 collective-permute-done.1
  17.2 5.3 %fusion.11 = bf16[321,1280]{1,0:T(8,128)(2,1)S(1)} fusion(bf16[384,1280]{1,0:T(8,128)(2,1)} %bitcast.51, f32[1280]{0:T(1024)} %param.15, pred[321]{0:T(512)(128)(4,1)S(1)} %fusion.67, bf16[2,128]{1,0:T(2,128)(2,1)S(1)} %collective-permute-done.1, bf16[320,128]{1,0:T(8,128)(2,1)} %param.12, bf16[2,128]{1,0:T(2,128)(2,1)S(1)} %collective-permute-done, ...), kind=kOutput, calls=%fused_computation.17 | convolution fusion | flops 344317440 | bytes 1975361 | tf_op jit(solution)/shard_map/dot_general | solution.py:71
  22.5 0.9 copy-done.3
  23.4 1.0 slice.62
  24.4 4.8 %slice.54 = bf16[160,1280]{1,0:T(8,128)(2,1)} slice(bf16[321,1280]{1,0:T(8,128)(2,1)} %copy-done.3), slice={[2:321:2], [0:1280:1]} | slice | bytes 819200 | tf_op jit(solution)/shard_map/slice | solution.py:76
  29.2 2.9 reshape.72
  32.1 2.8 fusion.73
  35.0 0.1 copy_bitcast_fusion
  35.1 0.8 copy-done.4
  36.0 0.1 copy-done.5
  36.1 0.1 copy-done.6
  36.2 7.7 %convert_reduce_fusion = (f32[160]{0:T(256)S(1)}, bf16[160,1280]{1,0:T(8,128)(2,1)S(1)}) fusion(f32[160,640]{1,0:T(8,128)S(1)} %copy-done.5, f32[160,640]{1,0:T(8,128)S(1)} %copy-done.4, f32[1280]{0:T(1024)S(1)} %copy-done.11, bf16[3840,1280]{1,0:T(8,128)(2,1)} %bitcast.50, bf16[160,1280]{1,0:T(8,128)(2,1)S(1)} %copy-done.6, ...), kind=kOutput, calls=%fused_computation.43 | convolution fusion | flops 1590886272 | bytes 12293760 | tf_op jit(solution)/shard_map/dot_general | solution.py:78
  44.0 0.3 fusion.32
  44.3 1.9 fusion.54
  46.2 1.4 copy-done.1
  47.6 0.8 slice.79
  48.5 0.0 all-gather.5.cloned.1.call-start
  48.6 2.4 fusion.42
  51.7 2.1 copy.20
  53.8 174.8 %all-gather.3.cloned.1.call-done = bf16[5120,1280]{1,0:T(8,128)(2,1)} async-done(((bf16[160,1280]{1,0:T(8,128)(2,1)}), bf16[5120,1280]{1,0:T(8,128)(2,1)}) %all-gather.3.cloned.1.call-update) | async-done | bytes 13107216 | tf_op jit(solution)/shard_map/all_gather | solution.py:105
  228.6 17.7 %copy.19 = bf16[5120,1280]{0,1:T(8,128)(2,1)} copy(bf16[5120,1280]{1,0:T(8,128)(2,1)} %all-gather.3.cloned.1.call-done) | data formatting | bytes 26214400 | tf_op jit(solution)/shard_map/all_gather | solution.py:105
  246.3 27.6 %bitcast_reduce_fusion = (f32[160,20]{0,1:T(8,128)S(1)}, f32[20,5120,160]{1,2,0:T(8,128)}) fusion(pred[5120]{0:T(1024)(128)(4,1)S(1)} %iota_compare_fusion, bf16[5120,20,64]{0,2,1:T(8,128)(2,1)} %bitcast.44, bf16[160,20,64]{0,2,1:T(8,128)(2,1)} %bitcast.48), kind=kOutput, calls=%fused_computation.1 | convolution fusion | flops 2146300800 | bytes 79070720 | tf_op jit(solution)/shard_map/qhd,khd->qhk/dot_general | solution.py:110
  273.9 21.5 %fusion.2 = f32[160,20]{0,1:T(8,128)S(1)} fusion(f32[20,5120,160]{1,2,0:T(8,128)} %get-tuple-element.19, f32[160,20]{0,1:T(8,128)S(1)} %get-tuple-element.13, pred[5120]{0:T(1024)(128)(4,1)S(1)} %iota_compare_fusion), kind=kLoop, calls=%fused_computation.5 | loop fusion | flops 81916800 | bytes 65566720 | tf_op jit(solution)/shard_map/reduce_sum | solution.py:122
  295.4 109.9 %all-gather.5.cloned.1.call-done = bf16[5120,1280]{1,0:T(8,128)(2,1)} async-done(((bf16[160,1280]{1,0:T(8,128)(2,1)}), bf16[5120,1280]{1,0:T(8,128)(2,1)}) %all-gather.5.cloned.1.call-update) | async-done | bytes 13107216 | tf_op jit(solution)/shard_map/all_gather | solution.py:106
  405.4 17.6 %copy.21 = bf16[5120,1280]{0,1:T(8,128)(2,1)} copy(bf16[5120,1280]{1,0:T(8,128)(2,1)} %all-gather.5.cloned.1.call-done) | data formatting | bytes 26214400 | tf_op jit(solution)/shard_map/all_gather | solution.py:106
  423.0 28.5 %divide_convert_fusion = bf16[160,20,64]{0,2,1:T(8,128)(2,1)} fusion(bf16[5120,20,64]{0,2,1:T(8,128)(2,1)} %bitcast.47, f32[20,5120,160]{1,2,0:T(8,128)} %get-tuple-element.19, f32[160,20]{0,1:T(8,128)S(1)} %get-tuple-element.13, pred[5120]{0:T(1024)(128)(4,1)S(1)} %iota_compare_fusion, f32[160,20]{0,1:T(8,128)S(1)} %fusion.2, ...), kind=kOutput, calls=%fused_computation.35 | convolution fusion | flops 2179686400 | bytes 79096320 | tf_op jit(solution)/shard_map/qhk,khd->qhd/dot_general | solution.py:123
  451.6 2.8 fusion.40
  (38 shorter events, 0.2 us)
Async XLA Ops:
  7.2 444.4 %copy-start = (bf16[1280,1280]{1,0:T(8,128)(2,1)S(1)}, bf16[1280,1280]{1,0:T(8,128)(2,1)}, u32[]{:S(2)}) copy-start(bf16[1280,1280]{1,0:T(8,128)(2,1)} %param.22) | copy-start | bytes 9830404
  7.2 221.4 %all-gather.3.cloned.1.call-start = ((), (), s32[]{:S(2)}) async-start(), calls=%async_computation | async-start | bytes 13516800 | tf_op jit(solution)/shard_map/all_gather | solution.py:105
  8.1 7.3 %collective-permute-start = (bf16[2,128]{1,0:T(2,128)(2,1)S(1)}, bf16[2,128]{1,0:T(2,128)(2,1)S(1)}, u32[]{:S(2)}, u32[]{:S(2)}) collective-permute-start(bf16[2,128]{1,0:T(2,128)(2,1)S(1)} %get-tuple-element.10), channel_id=1, source_target_pairs={{0,1},{1,2},{2,3},{3,4},{4,5},{5,6},{6,7},{7,8},{8,9},{9,10},{10,1... | collective-permute-start | bytes 1544 | tf_op jit(solution)/shard_map/ppermute | solution.py:23
  11.7 5.5 %collective-permute-start.1 = (bf16[2,128]{1,0:T(2,128)(2,1)S(1)}, bf16[2,128]{1,0:T(2,128)(2,1)S(1)}, u32[]{:S(2)}, u32[]{:S(2)}) collective-permute-start(bf16[2,128]{1,0:T(2,128)(2,1)S(1)} %get-tuple-element.11), channel_id=1, source_target_pairs={{1,0},{2,1},{3,2},{4,3},{5,4},{6,5},{7,6},{8,7},{9,8},{10,9},{11,1... | collective-permute-start | bytes 1544 | tf_op jit(solution)/shard_map/ppermute | solution.py:25
  22.5 0.9 copy-start.3
  35.0 1.0 copy-start.4
  35.0 1.1 copy-start.5
  35.0 1.2 copy-start.6
  35.0 1.2 copy-start.11
  35.0 9.3 %slice-start = ((s8[9830400]{0:T(1024)(128)(4,1)}), s8[4194304]{0:T(1024)(128)(4,1)S(1)}, s32[]{:S(2)}) async-start(s8[9830400]{0:T(1024)(128)(4,1)} %bitcast.45), calls=%async_computation.2 | async-start | bytes 8388608
  36.2 8.1 %slice-start.1 = ((s8[9830400]{0:T(1024)(128)(4,1)}), s8[4194304]{0:T(1024)(128)(4,1)S(1)}, s32[]{:S(2)}) async-start(s8[9830400]{0:T(1024)(128)(4,1)} %bitcast.45), calls=%async_computation.3 | async-start | bytes 8388608
  36.2 8.1 %slice-start.2 = ((s8[9830400]{0:T(1024)(128)(4,1)}), s8[1441792]{0:T(1024)(128)(4,1)S(1)}, s32[]{:S(2)}) async-start(s8[9830400]{0:T(1024)(128)(4,1)} %bitcast.45), calls=%async_computation.4 | async-start | bytes 2883584
  36.2 8.1 %copy-start.7 = (f32[1280]{0:T(1024)S(1)}, f32[1280]{0:T(1024)}, u32[]{:S(2)}) copy-start(f32[1280]{0:T(1024)} %param.19) | copy-start | bytes 15364
  36.2 8.1 %copy-start.8 = (f32[1280]{0:T(1024)S(1)}, f32[1280]{0:T(1024)}, u32[]{:S(2)}) copy-start(f32[1280]{0:T(1024)} %param.18) | copy-start | bytes 15364
  44.0 2.2 copy-start.2
  44.3 4.2 copy-start.9
  46.2 1.4 copy-start.1
  48.5 356.9 %all-gather.5.cloned.1.call-start = ((), (), s32[]{:S(2)}) async-start(), calls=%async_computation.1 | async-start | bytes 13516800 | tf_op jit(solution)/shard_map/all_gather | solution.py:106
  423.0 28.5 %copy-start.10 = (f32[1280]{0:T(1024)S(1)}, f32[1280]{0:T(1024)}, u32[]{:S(2)}) copy-start(f32[1280]{0:T(1024)} %param.23) | copy-start | bytes 15364
Sparse Core Ops, SparseCore 0:
  48.6 179.9 all-gather.2
  230.2 175.1 all-gather.4
where the time goes:
time: 463 us; the launch traced here: 461 us
  waiting for transfers between devices  286 us (62%)
  matrix products  73.9 us (16%)
  local copies, waits for them, and re-layouts  54.3 us (12%)
  other arithmetic  27.6 us (6%)
  between operations  15 us (3%)
  starting transfers between devices  5 us (1%)
    all_gather x1, waiting for transfers between devices, shards(): key_piece = lax.all_gather(key_rows, 'seq', axis=0, tiled=True)  175 us
    all_gather x1, waiting for transfers between devices, shards(): value_piece = lax.all_gather(values, 'seq', axis=0, tiled=True)  110 us
    dot_general x1, matrix products, shards(): jnp.einsum('qhk,khd->qhd', weights.astype(jnp.bfloat16), value_piece.resh...  28.5 us
    dot_general x1, matrix products, shards(): jnp.einsum('qhd,khd->qhk', query_heads, key_piece.reshape(piece_rows, hea...  27.6 us
    reduce_sum x1, other arithmetic, shards(): totals = jnp.sum(weights, axis=2)  21.5 us
    all_gather x1, local copies, waits for them, and re-layouts, shards(): key_piece = lax.all_gather(key_rows, 'seq', axis=0, tiled=True)  17.7 us
    all_gather x1, local copies, waits for them, and re-layouts, shards(): value_piece = lax.all_gather(values, 'seq', axis=0, tiled=True)  17.6 us
  transfers between devices with their start and end apart: 4, of which 3 were waited for; matrix products, arithmetic and copies ran while one was open for 16% of the time, Pallas kernels for 0%

commit v1 on v0

v1 whole, which is shorter than its diff:
```python
import math

import jax
import jax.numpy as jnp
from jax import lax
from jax.experimental import pallas as pl
from jax.experimental.pallas import tpu as pltpu
from jax.sharding import PartitionSpec as P

HEAD_DIM = 64
LANES = 128
GROUP = 8
norm_epsilon = 1e-05


def sinusoids(first_frame, frame_count, model_width):
    half_width = model_width // 2
    increment = math.log(10000.0) / (half_width - 1)
    inverse = jnp.exp(-increment * jnp.arange(half_width, dtype=jnp.float32))
    moments = (first_frame + jnp.arange(frame_count, dtype=jnp.int32)).astype(jnp.float32)
    angles = moments[:, None] * inverse[None, :]
    return jnp.concatenate([jnp.sin(angles), jnp.cos(angles)], axis=1)


def gelu(v):
    return 0.5 * v * (1.0 + lax.erf(v * (2.0**-0.5)))


def window(whole, rolled, start):
    if start % LANES == 0:
        return whole[:, start : start + LANES]
    return rolled[:, start - 64 : start + 64]


def ab_start(g):
    return 320 * (g // 2) + 192 * (g % 2)


def s_start(g):
    return 320 * (g // 2) + 128


def low_lanes(rows):
    return lax.broadcasted_iota(jnp.int32, (rows, LANES), 1) < 64


W2_PARTS = 6


def stem_kernel(
    first_ref, lhs_ref, pos_ref, b1_ref, b2_ref, gain_ref, nbias_ref, vbias_ref,
    w1_hbm, w2_hbm, wp_hbm,
    kv_ref, normed_ref, stem_ref,
    w1, w2, wkv, odd, sems,
):
    frames, width = stem_ref.shape
    part = w2.shape[0] // W2_PARTS
    c1 = pltpu.make_async_copy(w1_hbm, w1, sems.at[0])
    c1.start()
    c2 = []
    for i in range(W2_PARTS):
        rows = pl.ds(i * part, part)
        c2.append(pltpu.make_async_copy(w2_hbm.at[rows], w2.at[rows], sems.at[1 + i]))
        c2[-1].start()
    c3 = []
    for i in range(2):
        c3.append(
            pltpu.make_async_copy(
                wp_hbm.at[:, pl.ds(width * (1 + i), width)],
                wkv.at[:, pl.ds(width * i, width)],
                sems.at[1 + W2_PARTS + i],
            )
        )
        c3[-1].start()
    c1.wait()
    pad = lhs_ref.shape[0] - frames
    first = gelu(jnp.dot(lhs_ref[...], w1[...], preferred_element_type=jnp.float32) + b1_ref[...])
    row = lax.broadcasted_iota(jnp.int32, (pad, width), 0)
    dead = jnp.logical_and(row == 0, first_ref[0] != 0)
    odd[...] = jnp.where(dead, 0.0, first[:pad])
    before = odd[0:frames, :].astype(jnp.bfloat16)
    after = odd[1 : frames + 1, :].astype(jnp.bfloat16)
    even = first[pad:].astype(jnp.bfloat16)
    total = None
    per = W2_PARTS // 3
    for tap, rows in enumerate((before, even, after)):
        for i in range(per):
            c2[tap * per + i].wait()
            term = jnp.dot(
                rows[:, i * part : (i + 1) * part],
                w2[(tap * per + i) * part : (tap * per + i + 1) * part, :],
                preferred_element_type=jnp.float32,
            )
            total = term if total is None else total + term
    second = gelu(total + b2_ref[...])
    stem = (second + pos_ref[...]).astype(jnp.bfloat16)
    stem_ref[...] = stem
    wide = stem.astype(jnp.float32)
    centred = wide - jnp.mean(wide, axis=1, keepdims=True)
    spread = jnp.mean(centred * centred, axis=1, keepdims=True)
    normed = (centred * lax.rsqrt(spread + norm_epsilon) * gain_ref[...] + nbias_ref[...]).astype(jnp.bfloat16)
    normed_ref[...] = normed
    c3[0].wait()
    keys = jnp.dot(normed, wkv[:, :width], preferred_element_type=jnp.float32)
    c3[1].wait()
    values = jnp.dot(normed, wkv[:, width:], preferred_element_type=jnp.float32) + vbias_ref[...]
    keys_r = pltpu.roll(keys, width - 64, 1)
    values_r = pltpu.roll(values, width - 64, 1)
    low = low_lanes(frames)
    for g in range(GROUP):
        kv_ref[g, 0:frames, :] = window(keys, keys_r, ab_start(g)).astype(jnp.bfloat16)
        kv_ref[g, frames : 2 * frames, :] = window(values, values_r, ab_start(g)).astype(jnp.bfloat16)
        shared = jnp.where(low, window(keys, keys_r, s_start(g)), window(values, values_r, s_start(g) - 64))
        kv_ref[g, 2 * frames : 3 * frames, :] = shared.astype(jnp.bfloat16)


def query_kernel(normed_ref, bias_ref, w_ref, q_ref):
    frames, width = normed_ref.shape
    half = frames // 2
    scale = HEAD_DIM**-0.5 * math.log2(math.e)
    q = (jnp.dot(normed_ref[...], w_ref[...], preferred_element_type=jnp.float32) + bias_ref[...]) * scale
    q_r = pltpu.roll(q, width - 64, 1)
    low = low_lanes(half)
    for g in range(GROUP):
        q_ref[g, 0:frames, :] = window(q, q_r, ab_start(g)).astype(jnp.bfloat16)
        rows = slice(half * (g % 2), half * (g % 2 + 1))
        shared = window(q, q_r, s_start(g))[rows]
        q_ref[g, frames : frames + half, :] = jnp.where(low, shared, 0.0).astype(jnp.bfloat16)


NEG = -1e30
STEP = 2


def attend_kernel(*refs, chunks, opening, closing):
    refs = list(refs)
    info = refs.pop(0)
    q_ref = refs.pop(0)
    kv_refs = [refs.pop(0) for _ in range(chunks)]
    if opening:
        old = None
    else:
        old = [refs.pop(0) for _ in range(3)]
    if closing:
        o_ref = refs.pop(0)
        state = [refs.pop(0) for _ in range(3)]
    else:
        state = [refs.pop(0) for _ in range(3)]
    k_ab, v_ab, k_s, v_s = refs
    m_ref, l_ref, a_ref = state
    span = k_ab.shape[0]
    frames = kv_refs[0].shape[1] // 3
    half = frames // 2
    if opening:
        m_ref[...] = jnp.full(m_ref.shape, NEG, jnp.float32)
        l_ref[...] = jnp.zeros(l_ref.shape, jnp.float32)
        a_ref[...] = jnp.zeros(a_ref.shape, jnp.float32)
    else:
        for new, was in zip(state, old):
            new[...] = was[...]

    def update(q, k, v, m_old):
        s = lax.dot_general(q, k, (((1,), (1,)), ((), ())), preferred_element_type=jnp.float32)
        m_new = jnp.maximum(m_old, jnp.max(s, axis=1, keepdims=True))
        p = jnp.exp2(s - m_new).astype(jnp.bfloat16)
        out = jnp.dot(p, v, preferred_element_type=jnp.float32)
        return m_new, out

    for c in range(chunks):
        live = info[0] - info[1 + c]

        @pl.when(live > 0)
        def _():
            kv = kv_refs[c]
            alive = lax.broadcasted_iota(jnp.int32, (span, LANES), 0) < live

            def put(ref, lanes, got):
                ref[:, lanes] = got.astype(jnp.bfloat16)

            ones = jnp.where(alive, 1.0, 0.0)
            kab = kv[:, 0:frames, :].reshape(span, LANES).astype(jnp.float32)
            vab = kv[:, frames : 2 * frames, :].reshape(span, LANES).astype(jnp.float32)
            sh = kv[:, 2 * frames : 3 * frames, :].reshape(span, LANES).astype(jnp.float32)
            put(k_ab, slice(0, LANES), jnp.where(alive, kab, kab[0:1]))
            put(v_ab, slice(0, LANES), jnp.where(alive, vab, 0.0))
            put(v_ab, slice(LANES, 2 * LANES), ones)
            put(k_s, slice(0, LANES), jnp.where(alive, sh, sh[0:1]))
            put(v_s, slice(0, LANES), jnp.where(alive, sh, 0.0))
            put(v_s, slice(LANES, 2 * LANES), ones)

            def step(i, carry):
                rows = STEP * frames
                at = pl.ds(pl.multiple_of(i * rows, rows), rows)
                q = q_ref[pl.ds(i * STEP, STEP), 0:frames, :].reshape(rows, LANES)
                low = low_lanes(rows)
                zero = jnp.zeros_like(q)
                qq = jnp.concatenate([jnp.where(low, q, zero), jnp.where(low, zero, q)], axis=0)
                m = m_ref[at, :]
                m_new, out = update(qq, k_ab[...], v_ab[...], jnp.concatenate([m[:, 0:1], m[:, 64:65]], axis=0))
                m_two = jnp.where(low, m_new[:rows], m_new[rows:])
                keep = jnp.exp2(m - m_two)
                m_ref[at, :] = m_two
                a_ref[at, :] = a_ref[at, :] * keep + jnp.where(low, out[:rows, :LANES], out[rows:, :LANES])
                l_ref[at, :] = l_ref[at, :] * keep + jnp.where(low, out[:rows, LANES:], out[rows:, LANES:])
                few = STEP * half
                at = pl.ds(pl.multiple_of(GROUP * frames + i * few, few), few)
                qs = q_ref[pl.ds(i * STEP, STEP), frames : frames + half, :].reshape(few, LANES)
                m = m_ref[at, :]
                m_new, out = update(qs, k_s[...], v_s[...], m[:, 0:1])
                m_two = jnp.broadcast_to(m_new, m.shape)
                keep = jnp.exp2(m - m_two)
                m_ref[at, :] = m_two
                a_ref[at, :] = a_ref[at, :] * keep + out[:, :LANES]
                l_ref[at, :] = l_ref[at, :] * keep + out[:, LANES:]
                return carry

            lax.fori_loop(0, GROUP // STEP, step, 0)

    if closing:
        cut = GROUP * frames
        o_ref[:, 0:frames, :] = (a_ref[0:cut, :] / l_ref[0:cut, :]).astype(jnp.bfloat16).reshape(GROUP, frames, LANES)
        rest = jnp.where(low_lanes(GROUP * half), 0.0, a_ref[cut:, :] / l_ref[cut:, :])
        o_ref[:, frames : frames + half, :] = rest.astype(jnp.bfloat16).reshape(GROUP, half, LANES)


def output_kernel(o_ref, w_ref, bias_ref, stem_ref, attended_ref, encoded_ref):
    frames, width = stem_ref.shape
    half = frames // 2
    total = None
    for g in range(GROUP):
        at = ab_start(g)
        term = jnp.dot(o_ref[g, 0:frames, :], w_ref[at : at + LANES, :], preferred_element_type=jnp.float32)
        total = term if total is None else total + term
        if g % 2:
            at = s_start(g) - 64
            shared = jnp.concatenate(
                [o_ref[g - 1, frames : frames + half, :], o_ref[g, frames : frames + half, :]], axis=0
            )
            total = total + jnp.dot(shared, w_ref[at : at + LANES, :], preferred_element_type=jnp.float32)
    total = total + bias_ref[...]
    attended_ref[...] = total.astype(jnp.bfloat16)
    encoded_ref[...] = (stem_ref[...].astype(jnp.float32) + total).astype(jnp.bfloat16)


VMEM = pltpu.MemorySpace.VMEM
SMEM = pltpu.MemorySpace.SMEM


def spec(space):
    return pl.BlockSpec(memory_space=space)


def params(mib):
    return pltpu.CompilerParams(vmem_limit_bytes=mib * 2**20)


def shards(
    spectrum, valid_frames, inlet_weight, inlet_bias, stride_weight, stride_bias, norm_gain, norm_bias,
    projection_weight, query_value_bias, out_weight, out_bias,
):
    mel_rows, channels = spectrum.shape
    frames = mel_rows // 2
    width = projection_weight.shape[0]
    count = lax.axis_size("seq")
    me = lax.axis_index("seq")
    pairs = spectrum.reshape(frames, 2 * channels)
    down = [(i, i + 1) for i in range(count - 1)]
    up = [(i + 1, i) for i in range(count - 1)]
    earlier = lax.ppermute(pairs[frames - 1 :], "seq", down)
    later = lax.ppermute(pairs[:1], "seq", up)
    wide = jnp.concatenate([earlier, pairs, later], axis=0)
    odd_rows = jnp.concatenate([wide[0 : frames + 1], wide[1 : frames + 2, :channels]], axis=1)
    even_rows = jnp.concatenate([wide[0:frames, channels:], wide[1 : frames + 1]], axis=1)
    pad = 16
    lhs = jnp.concatenate([jnp.pad(odd_rows, ((0, pad - 1), (0, 0))), even_rows], axis=0)
    position = sinusoids(me * frames, frames, width)
    first = (me == 0).astype(jnp.int32).reshape(1)
    row = lambda v: v.reshape(1, width)
    bf16 = lambda *dims: jax.ShapeDtypeStruct(dims, jnp.bfloat16)
    f32 = lambda *dims: jax.ShapeDtypeStruct(dims, jnp.float32)

    kv, normed, stem = pl.pallas_call(
        stem_kernel,
        name="stem",
        out_shape=(bf16(GROUP, 3 * frames, LANES), bf16(frames, width), bf16(frames, width)),
        in_specs=[spec(SMEM)] + [spec(VMEM)] * 7 + [spec(pltpu.MemorySpace.HBM)] * 3,
        out_specs=(spec(VMEM),) * 3,
        scratch_shapes=[
            pltpu.VMEM((3 * channels, width), jnp.bfloat16),
            pltpu.VMEM((3 * width, width), jnp.bfloat16),
            pltpu.VMEM((width, 2 * width), jnp.bfloat16),
            pltpu.VMEM((frames + pad, width), jnp.float32),
            pltpu.SemaphoreType.DMA((3 + W2_PARTS,)),
        ],
        compiler_params=params(40),
        cost_estimate=pl.CostEstimate(flops=4 * 10**9, bytes_accessed=20 * 10**6, transcendentals=0),
    )(
        first, lhs, position, row(inlet_bias), row(stride_bias), row(norm_gain), row(norm_bias),
        row(query_value_bias[1]),
        inlet_weight.reshape(3 * channels, width), stride_weight.reshape(3 * width, width), projection_weight,
    )

    teams = [list(range(i, i + GROUP)) for i in range(0, count, GROUP)]
    swap = lambda v: lax.all_to_all(v, "seq", 0, 0, axis_index_groups=teams)
    kv = swap(kv)
    spans = count // GROUP
    shift = lambda v, by: lax.ppermute(v, "seq", [(i, (i + by * GROUP) % count) for i in range(count)])
    others = [shift(kv, by) for by in (1, spans - 1, 2)]

    query = pl.pallas_call(
        query_kernel,
        name="query",
        grid=(1,),
        out_shape=bf16(GROUP, frames + frames // 2, LANES),
        in_specs=[
            pl.BlockSpec((frames, width), lambda i: (0, 0)),
            pl.BlockSpec((1, width), lambda i: (0, 0)),
            pl.BlockSpec((width, width), lambda i: (0, 0)),
        ],
        out_specs=pl.BlockSpec((GROUP, frames + frames // 2, LANES), lambda i: (0, 0, 0)),
        compiler_params=params(20),
        cost_estimate=pl.CostEstimate(flops=10**9, bytes_accessed=4 * 10**6, transcendentals=0),
    )(normed, row(query_value_bias[0]), projection_weight)
    query = swap(query)

    live = valid_frames[0]
    mine = me // GROUP
    span = GROUP * frames
    rows = span + span // 2
    scratch = [
        pltpu.VMEM((span, LANES), jnp.bfloat16),
        pltpu.VMEM((span, 2 * LANES), jnp.bfloat16),
        pltpu.VMEM((span, LANES), jnp.bfloat16),
        pltpu.VMEM((span, 2 * LANES), jnp.bfloat16),
    ]
    states = (f32(rows, LANES),) * 3

    def attend(blocks, steps, state, closing):
        info = jnp.stack([live] + [((mine - by) % spans) * span for by in steps]).astype(jnp.int32)
        operands = [info, query, *blocks, *(state or ())]
        out = (bf16(GROUP, frames + frames // 2, LANES),) if closing else states
        body = lambda *refs: attend_kernel(*refs, chunks=len(blocks), opening=state is None, closing=closing)
        extra = [pltpu.VMEM((rows, LANES), jnp.float32)] * 3 if closing else []
        return pl.pallas_call(
            body,
            name="attend%d" % len(blocks) + ("z" if closing else ""),
            out_shape=out,
            in_specs=[spec(SMEM)] + [spec(VMEM)] * (len(operands) - 1),
            out_specs=tuple(spec(VMEM) for _ in out),
            scratch_shapes=extra + scratch,
            compiler_params=params(40),
            cost_estimate=pl.CostEstimate(flops=4 * 10**9 * len(blocks), bytes_accessed=5 * 10**6, transcendentals=0),
        )(*operands)

    state = attend([kv], [0], None, False)
    state = attend(others[:2], [1, spans - 1], state, False)
    (mixed,) = attend(others[2:], [2], state, True)
    mixed = swap(mixed)
    attended, encoded = pl.pallas_call(
        output_kernel,
        name="output",
        out_shape=(bf16(frames, width),) * 2,
        in_specs=[spec(VMEM)] * 4,
        out_specs=(spec(VMEM),) * 2,
        compiler_params=params(20),
        cost_estimate=pl.CostEstimate(flops=10**9, bytes_accessed=4 * 10**6, transcendentals=0),
    )(mixed, out_weight, row(out_bias), stem)
    return attended, encoded


def solution(mesh):
    in_specs = (P(("dp", "seq"), None), P("dp"), P(), P(), P(), P(), P(), P(), P(), P(), P(), P())
    out_specs = (P(("dp", "seq"), None), P(("dp", "seq"), None))
    return jax.shard_map(shards, mesh=mesh, in_specs=in_specs, out_specs=out_specs, check_vma=False)
```

time: 463 us -> 145 us (0.31)
  the two profiles are of different devices: /device:TPU:0 before, /device:TPU:88 now
where the time goes in v1:
time: 145 us; the launch traced here: 144 us
  Pallas kernels  56.7 us (39%)
  waiting for transfers between devices  32.6 us (22%)
  starting transfers between devices  19.7 us (14%)
  blocking collectives  17.8 us (12%)
  local copies, waits for them, and re-layouts  13.4 us (9%)
  other arithmetic  1.85 us (1%)
  between operations  1.58 us (1%)
    pallas_call x3, Pallas kernels, attend(): pl.pallas_call(body, name='attend%d' % len(blocks) + ('z' if closing else...  44.5 us
    all_to_all x1, blocking collectives, shards(): swap = lambda v: lax.all_to_all(v, 'seq', 0, 0, axis_index_groups=teams)  17.8 us
    ppermute x3, waiting for transfers between devices, shards(): lax.ppermute(v, 'seq', [(i, (i + by * GROUP) % count) for i in range(coun...  17.8 us
    all_to_all x2, waiting for transfers between devices, shards(): swap = lambda v: lax.all_to_all(v, 'seq', 0, 0, axis_index_groups=teams)  14.8 us
    unnamed x27, local copies, waits for them, and re-layouts  8.91 us
    all_to_all x2, starting transfers between devices, shards(): swap = lambda v: lax.all_to_all(v, 'seq', 0, 0, axis_index_groups=teams)  7.61 us
    pallas_call x1, Pallas kernels, shards(): pl.pallas_call(stem_kernel, name='stem', out_shape=(bf16(GROUP, 3 * frame...  7.29 us
    ppermute x1, starting transfers between devices, shards(): later = lax.ppermute(pairs[:1], 'seq', up)  5.45 us
  transfers between devices with their start and end apart: 7, of which 3 were waited for; matrix products, arithmetic and copies ran while one was open for 4% of the time, Pallas kernels for 24%

profile of v1, /device:TPU:88, one launch (start us, length us, event | category | flops | bytes accessed | tf_op | source)
XLA Modules:
  0.0 143.7 jit_solution(6951943340415136971)
XLA Ops:
  0.6 0.7 slice_bitcast_fusion
  1.3 3.4 %collective-permute-start = (bf16[1,256]{1,0:T(2,128)(2,1)S(1)}, bf16[1,256]{1,0:T(2,128)(2,1)S(1)}, u32[]{:S(2)}, u32[]{:S(2)}) collective-permute-start(bf16[1,256]{1,0:T(2,128)(2,1)S(1)} %bitcast.23), channel_id=1, source_target_pairs={{0,1},{1,2},{2,3},{3,4},{4,5},{5,6},{6,7},{7,8},{8,9},{9,10},{10,1... | collective-permute-start | bytes 1544 | tf_op jit(solution)/shard_map/ppermute | solution.py:269
  4.8 5.5 %collective-permute-start.1 = (bf16[1,256]{1,0:T(2,128)(2,1)S(1)}, bf16[1,256]{1,0:T(2,128)(2,1)S(1)}, u32[]{:S(2)}, u32[]{:S(2)}) collective-permute-start(bf16[1,256]{1,0:T(2,128)(2,1)S(1)} %bitcast.24), channel_id=1, source_target_pairs={{1,0},{2,1},{3,2},{4,3},{5,4},{6,5},{7,6},{8,7},{9,8},{10,9},{11,1... | collective-permute-start | bytes 1544 | tf_op jit(solution)/shard_map/ppermute | solution.py:270
  10.2 0.9 reshape.47
  11.2 0.8 fusion.9
  12.0 1.5 %multiply_sine_fusion = (f32[160,640]{1,0:T(8,128)S(1)}, f32[160,640]{1,0:T(8,128)S(1)}) fusion(f32[640]{0:T(1024)S(1)} %multiply_exponential_fusion, f32[160]{0:T(256)S(1)} %add_convert_fusion), kind=kLoop, calls=%fused_computation.2 | loop fusion | flops 102400 | bytes 822400 | tf_op jit(solution)/shard_map/sin | solution.py:22
  13.5 0.7 reshape.48.b1_ref
  14.2 0.7 reshape.49.b2_ref
  14.9 0.7 reshape.50.gain_ref
  15.6 0.7 reshape.51.nbias_ref
  16.4 3.9 %copy-done = bf16[3,1280,1280]{2,1,0:T(8,128)(2,1)S(1)} copy-done((bf16[3,1280,1280]{2,1,0:T(8,128)(2,1)S(1)}, bf16[3,1280,1280]{2,1,0:T(8,128)(2,1)}, u32[]{:S(2)}) %copy-start) | copy-done | bytes 9830424
  20.4 1.3 copy-done.2
  21.6 7.3 %stem.1 = (bf16[8,480,128]{2,1,0:T(8,128)(2,1)S(1)}, bf16[160,1280]{1,0:T(8,128)(2,1)S(1)}, bf16[160,1280]{1,0:T(8,128)(2,1)S(1)}) custom-call(s32[1]{0:T(128)} %bitcast.1.first_ref, bf16[336,384]{1,0:T(8,128)(2,1)S(1)} %fusion.5.lhs_ref, f32[160,1280]{1,0:T(8,128)S(1)} %pad_maximum_fusion.pos_ref, f32[1,1280]{1,0:T(1,128)S(1)} %reshape.48.b1_ref, ...), custom_call_target="tpu_custom_call" | custom-call | flops 4000000000 | bytes 20000000 | tf_op jit(solution)/shard_map/stem/pallas_call | solution.py:282
  29.0 17.8 %all_to_all.15.refs_2_ = bf16[8,480,128]{2,1,0:T(8,128)(2,1)} all-to-all(bf16[8,480,128]{2,1,0:T(8,128)(2,1)S(1)} %get-tuple-element.12), channel_id=1, replica_groups={{0,1,2,3,4,5,6,7},{8,9,10,11,12,13,14,15},{16,17,18,19,20,21,22,23},{24..., dimensions={0} | all-to-all | bytes 1966080 | tf_op jit(solution)/shard_map/all_to_all | solution.py:304
  46.8 2.0 %collective-permute-start.4 = (bf16[8,480,128]{2,1,0:T(8,128)(2,1)}, bf16[8,480,128]{2,1,0:T(8,128)(2,1)}, u32[]{:S(2)}, u32[]{:S(2)}) collective-permute-start(bf16[8,480,128]{2,1,0:T(8,128)(2,1)} %all_to_all.15.refs_2_), channel_id=1, source_target_pairs={{0,24},{1,25},{2,26},{3,27},{4,28},{5,29},{6,30},{7,31},{8,0},{9,1... | collective-permute-start | bytes 2949128 | tf_op jit(solution)/shard_map/ppermute | solution.py:307
  48.8 1.6 %query.1 = bf16[8,240,128]{2,1,0:T(8,128)(2,1)} custom-call(bf16[160,1280]{1,0:T(8,128)(2,1)S(1)} %get-tuple-element.11.normed_ref, f32[1,1280]{1,0:T(1,128)S(1)} %get-tuple-element.22.bias_ref, bf16[1280,3840]{1,0:T(8,128)(2,1)S(1)} %bitcast.20), custom_call_target="tpu_custom_call" | custom-call | flops 1000000000 | bytes 4000000 | tf_op jit(solution)/shard_map/query/pallas_call | solution.py:310
  50.4 3.5 %all-to-all-start = ((bf16[8,240,128]{2,1,0:T(8,128)(2,1)}), bf16[8,240,128]{2,1,0:T(8,128)(2,1)S(1)}, u32[]{:S(2)}, u32[]{:S(2)}) async-start(bf16[8,240,128]{2,1,0:T(8,128)(2,1)} %query.1), calls=%async_computation | async-start | bytes 983040 | tf_op jit(solution)/shard_map/all_to_all | solution.py:304
  54.6 0.1 pad_add_fusion.refs_0_
  54.7 0.1 pad_add_fusion.2.refs_0_
  54.8 0.1 pad_add_fusion.1.refs_0_
  54.8 1.3 collective-permute-start.2
  56.1 6.2 %all-to-all-done.refs_1_ = bf16[8,240,128]{2,1,0:T(8,128)(2,1)S(1)} async-done(((bf16[8,240,128]{2,1,0:T(8,128)(2,1)}), bf16[8,240,128]{2,1,0:T(8,128)(2,1)S(1)}, u32[]{:S(2)}, u32[]{:S(2)}) %all-to-all-start) | async-done | bytes 491552 | tf_op jit(solution)/shard_map/all_to_all | solution.py:304
  62.3 11.5 %attend1.1 = (f32[1920,128]{1,0:T(8,128)S(1)}, f32[1920,128]{1,0:T(8,128)S(1)}, f32[1920,128]{1,0:T(8,128)S(1)}) custom-call(s32[2]{0:T(128)S(1)} %pad_add_fusion.2.refs_0_, bf16[8,240,128]{2,1,0:T(8,128)(2,1)S(1)} %all-to-all-done.refs_1_, bf16[8,480,128]{2,1,0:T(8,128)(2,1)} %all_to_all.15.refs_2_), custom_call_target="tpu_custom_call" | custom-call | flops 4000000000 | bytes 5000000 | tf_op jit(solution)/shard_map/attend1/pallas_call | solution.py:344
  73.8 17.8 %collective-permute-done.4.refs_3_ = bf16[8,480,128]{2,1,0:T(8,128)(2,1)} collective-permute-done((bf16[8,480,128]{2,1,0:T(8,128)(2,1)}, bf16[8,480,128]{2,1,0:T(8,128)(2,1)}, u32[]{:S(2)}, u32[]{:S(2)}) %collective-permute-start.4) | collective-permute-done | bytes 983072 | tf_op jit(solution)/shard_map/ppermute | solution.py:307
  91.6 21.6 %attend2.1 = (f32[1920,128]{1,0:T(8,128)S(1)}, f32[1920,128]{1,0:T(8,128)S(1)}, f32[1920,128]{1,0:T(8,128)S(1)}) custom-call(s32[3]{0:T(128)S(1)} %pad_add_fusion.1.refs_0_, bf16[8,240,128]{2,1,0:T(8,128)(2,1)S(1)} %all-to-all-done.refs_1_, bf16[8,480,128]{2,1,0:T(8,128)(2,1)} %collective-permute-done.3.refs_2_, ...), custom_call_target="tpu_custom_call" | custom-call | flops 8000000000 | bytes 5000000 | tf_op jit(solution)/shard_map/attend2/pallas_call | solution.py:344
  113.3 1.2 copy-done.4
  114.5 11.3 %attend1z.1 = bf16[8,240,128]{2,1,0:T(8,128)(2,1)S(1)} custom-call(s32[2]{0:T(128)S(1)} %pad_add_fusion.refs_0_, bf16[8,240,128]{2,1,0:T(8,128)(2,1)S(1)} %copy-done.4, bf16[8,480,128]{2,1,0:T(8,128)(2,1)} %collective-permute-done.2.refs_2_, f32[1920,128]{1,0:T(8,128)S(1)} %get-tuple-element.16.refs_3_, f32[1920,128]{1,0:T(8,128)S(1)} %get-tuple-element.17.refs_4_, ...), custom_call_target="tpu_custom_call" | custom-call | flops 4000000000 | bytes 5000000 | tf_op jit(solution)/shard_map/attend1z/pallas_call | solution.py:344
  125.9 0.8 copy-done.5
  126.6 4.1 %all-to-all-start.2 = ((bf16[8,240,128]{2,1,0:T(8,128)(2,1)}), bf16[8,240,128]{2,1,0:T(8,128)(2,1)}, u32[]{:S(2)}, u32[]{:S(2)}) async-start(bf16[8,240,128]{2,1,0:T(8,128)(2,1)} %copy-done.5), calls=%async_computation.2 | async-start | bytes 983040 | tf_op jit(solution)/shard_map/all_to_all | solution.py:304
  130.8 8.5 %all-to-all-done.2.o_ref = bf16[8,240,128]{2,1,0:T(8,128)(2,1)} async-done(((bf16[8,240,128]{2,1,0:T(8,128)(2,1)}), bf16[8,240,128]{2,1,0:T(8,128)(2,1)}, u32[]{:S(2)}, u32[]{:S(2)}) %all-to-all-start.2) | async-done | bytes 491552 | tf_op jit(solution)/shard_map/all_to_all | solution.py:304
  139.3 1.0 copy-done.7
  140.3 3.3 %output.1 = (bf16[160,1280]{1,0:T(8,128)(2,1)}, bf16[160,1280]{1,0:T(8,128)(2,1)}) custom-call(bf16[8,240,128]{2,1,0:T(8,128)(2,1)} %all-to-all-done.2.o_ref, bf16[1280,1280]{1,0:T(8,128)(2,1)S(1)} %copy-done.1, f32[1,1280]{1,0:T(1,128)S(1)} %reshape.54.bias_ref, bf16[160,1280]{1,0:T(8,128)(2,1)S(1)} %copy-done.7), custom_call_target="tpu_custom_call" | custom-call | flops 1000000000 | bytes 4000000 | tf_op jit(solution)/shard_map/output/pallas_call | solution.py:359
  (33 shorter events, 0.2 us)
Async XLA Ops:
  1.3 15.0 %collective-permute-start = (bf16[1,256]{1,0:T(2,128)(2,1)S(1)}, bf16[1,256]{1,0:T(2,128)(2,1)S(1)}, u32[]{:S(2)}, u32[]{:S(2)}) collective-permute-start(bf16[1,256]{1,0:T(2,128)(2,1)S(1)} %bitcast.23), channel_id=1, source_target_pairs={{0,1},{1,2},{2,3},{3,4},{4,5},{5,6},{6,7},{7,8},{8,9},{9,10},{10,1... | collective-permute-start | bytes 1544 | tf_op jit(solution)/shard_map/ppermute | solution.py:269
  4.8 11.6 %collective-permute-start.1 = (bf16[1,256]{1,0:T(2,128)(2,1)S(1)}, bf16[1,256]{1,0:T(2,128)(2,1)S(1)}, u32[]{:S(2)}, u32[]{:S(2)}) collective-permute-start(bf16[1,256]{1,0:T(2,128)(2,1)S(1)} %bitcast.24), channel_id=1, source_target_pairs={{1,0},{2,1},{3,2},{4,3},{5,4},{6,5},{7,6},{8,7},{9,8},{10,9},{11,1... | collective-permute-start | bytes 1544 | tf_op jit(solution)/shard_map/ppermute | solution.py:270
  16.4 32.4 %slice-start = ((s8[9830400]{0:T(1024)(128)(4,1)}), s8[4194304]{0:T(1024)(128)(4,1)S(1)}, s32[]{:S(2)}) async-start(s8[9830400]{0:T(1024)(128)(4,1)} %bitcast.19), calls=%async_computation.3 | async-start | bytes 8388608
  16.4 3.9 %copy-start = (bf16[3,1280,1280]{2,1,0:T(8,128)(2,1)S(1)}, bf16[3,1280,1280]{2,1,0:T(8,128)(2,1)}, u32[]{:S(2)}) copy-start(bf16[3,1280,1280]{2,1,0:T(8,128)(2,1)} %param.16) | copy-start | bytes 29491204
  20.4 1.3 copy-start.2
  21.6 27.2 %slice-start.1 = ((s8[9830400]{0:T(1024)(128)(4,1)}), s8[4194304]{0:T(1024)(128)(4,1)S(1)}, s32[]{:S(2)}) async-start(s8[9830400]{0:T(1024)(128)(4,1)} %bitcast.19), calls=%async_computation.4 | async-start | bytes 8388608
  21.6 27.2 %slice-start.2 = ((s8[9830400]{0:T(1024)(128)(4,1)}), s8[1441792]{0:T(1024)(128)(4,1)S(1)}, s32[]{:S(2)}) async-start(s8[9830400]{0:T(1024)(128)(4,1)} %bitcast.19), calls=%async_computation.5 | async-start | bytes 2883584
  28.9 17.9 %copy-start.6 = (bf16[160,1280]{1,0:T(8,128)(2,1)}, bf16[160,1280]{1,0:T(8,128)(2,1)S(1)}, u32[]{:S(2)}) copy-start(bf16[160,1280]{1,0:T(8,128)(2,1)S(1)} %get-tuple-element.19.stem_ref) | copy-start | bytes 1228804
  46.8 27.0 %collective-permute-start.3 = (bf16[8,480,128]{2,1,0:T(8,128)(2,1)}, bf16[8,480,128]{2,1,0:T(8,128)(2,1)}, u32[]{:S(2)}, u32[]{:S(2)}) collective-permute-start(bf16[8,480,128]{2,1,0:T(8,128)(2,1)} %all_to_all.15.refs_2_), channel_id=1, source_target_pairs={{0,8},{1,9},{2,10},{3,11},{4,12},{5,13},{6,14},{7,15},{8,16},{9,17... | collective-permute-start | bytes 2949128 | tf_op jit(solution)/shard_map/ppermute | solution.py:307
  46.8 44.8 %collective-permute-start.4 = (bf16[8,480,128]{2,1,0:T(8,128)(2,1)}, bf16[8,480,128]{2,1,0:T(8,128)(2,1)}, u32[]{:S(2)}, u32[]{:S(2)}) collective-permute-start(bf16[8,480,128]{2,1,0:T(8,128)(2,1)} %all_to_all.15.refs_2_), channel_id=1, source_target_pairs={{0,24},{1,25},{2,26},{3,27},{4,28},{5,29},{6,30},{7,31},{8,0},{9,1... | collective-permute-start | bytes 2949128 | tf_op jit(solution)/shard_map/ppermute | solution.py:307
  50.4 11.9 %all-to-all-start = ((bf16[8,240,128]{2,1,0:T(8,128)(2,1)}), bf16[8,240,128]{2,1,0:T(8,128)(2,1)S(1)}, u32[]{:S(2)}, u32[]{:S(2)}) async-start(bf16[8,240,128]{2,1,0:T(8,128)(2,1)} %query.1), calls=%async_computation | async-start | bytes 983040 | tf_op jit(solution)/shard_map/all_to_all | solution.py:304
  54.8 58.5 %collective-permute-start.2 = (bf16[8,480,128]{2,1,0:T(8,128)(2,1)}, bf16[8,480,128]{2,1,0:T(8,128)(2,1)}, u32[]{:S(2)}, u32[]{:S(2)}) collective-permute-start(bf16[8,480,128]{2,1,0:T(8,128)(2,1)} %all_to_all.15.refs_2_), channel_id=1, source_target_pairs={{0,16},{1,17},{2,18},{3,19},{4,20},{5,21},{6,22},{7,23},{8,24},{9,... | collective-permute-start | bytes 2949128 | tf_op jit(solution)/shard_map/ppermute | solution.py:307
  62.3 29.3 %copy-start.3 = (bf16[8,240,128]{2,1,0:T(8,128)(2,1)}, bf16[8,240,128]{2,1,0:T(8,128)(2,1)S(1)}, u32[]{:S(2)}) copy-start(bf16[8,240,128]{2,1,0:T(8,128)(2,1)S(1)} %all-to-all-done.refs_1_) | copy-start | bytes 1474564
  91.6 39.1 %copy-start.8 = (f32[1280]{0:T(1024)S(1)}, f32[1280]{0:T(1024)}, u32[]{:S(2)}) copy-start(f32[1280]{0:T(1024)} %param.23) | copy-start | bytes 15364
  113.3 26.0 %copy-start.1 = (bf16[1280,1280]{1,0:T(8,128)(2,1)S(1)}, bf16[1280,1280]{1,0:T(8,128)(2,1)}, u32[]{:S(2)}) copy-start(bf16[1280,1280]{1,0:T(8,128)(2,1)} %w_ref.3) | copy-start | bytes 9830404
  113.3 1.2 copy-start.4
  125.9 0.8 copy-start.5
  126.6 12.7 %all-to-all-start.2 = ((bf16[8,240,128]{2,1,0:T(8,128)(2,1)}), bf16[8,240,128]{2,1,0:T(8,128)(2,1)}, u32[]{:S(2)}, u32[]{:S(2)}) async-start(bf16[8,240,128]{2,1,0:T(8,128)(2,1)} %copy-done.5), calls=%async_computation.2 | async-start | bytes 983040 | tf_op jit(solution)/shard_map/all_to_all | solution.py:304
  139.3 1.0 copy-start.7
